TPU v7x, 32 devices: a whole 2x2x4 slice. The times are simulated.
32 devices in a mesh: seq: 8 (over z, y), grp: 4 (over x, core).
Axes of the slice: x: 2, y: 2, z: 4, core: 2. Of those that a mesh axis runs over, the one named last changes fastest.
Arguments:
- query_nope: bfloat16 [4, 2, 128, 128], P(None, None, 'seq'), may hold values from -12.859821 to 12.859821
- query_rope: bfloat16 [4, 2, 128, 64], P(None, None, 'seq'), may hold values from -150 to 150
- latent_cache: bfloat16 [4, 8192, 576], P(None, ('seq', 'grp')), may hold values from -5 to 5
- lengths: int32 [4], replicated, may hold values from 4096 to 8192
- key_weight: bfloat16 [128, 128, 512], P('seq'), may hold values from -0.5 to 0.5
- value_weight: bfloat16 [128, 512, 128], P('seq'), may hold values from -0.25 to 0.25
- output_weight: bfloat16 [16384, 7168], P('seq', 'grp'), may hold values from -0.0625 to 0.0625
Outputs:
- mixed: bfloat16 [4, 2, 7168], P(None, None, ('grp', 'seq'))
All inputs are finite; a program needn't handle non-finite values.
Results may differ from a plain program's by a relative error of at most 0.0095.
Values may be sent and summed in bfloat16 or wider, within the bound.
No kernel may reach another device: no remote copies, remote signals or barrier semaphores. Data moves between devices by JAX's collectives and lax.ppermute only.
A program may use at most 64 MiB of HBM per device.

v0:
```python
import jax
import jax.numpy as jnp
from jax import lax
from jax.sharding import PartitionSpec as P

NEGATIVE = -1e30


def joined(part, axis, combine):
    gathered = jax.tree.map(lambda a: lax.all_gather(a, axis), part)

    def take(source):
        return jax.tree.map(lambda a: lax.dynamic_index_in_dim(a, source, 0, False), gathered)

    return lax.fori_loop(
        1, lax.axis_size(axis), lambda source, state: combine(state, take(source)), take(0)
    )


def shard_partial(queries, cache_block, limits, offset, factor, latent_width):
    raw_score = (
        jnp.einsum("bqhd,bpd->bqhp", queries, cache_block, preferred_element_type=jnp.float32)
        * factor
    )
    places = offset + lax.broadcasted_iota(jnp.int32, (1, 1, cache_block.shape[1]), 2)
    visible = places < limits[:, :, None]
    scores = jnp.where(visible[:, :, None, :], raw_score, NEGATIVE)
    maxima = jnp.max(scores, axis=-1)
    powers = jnp.exp(scores - maxima[..., None])
    totals = jnp.sum(powers, axis=-1)
    weights = powers.astype(jnp.bfloat16)
    summed = jnp.einsum(
        "bqhp,bpd->bqhd",
        weights,
        cache_block[:, :, :latent_width],
        preferred_element_type=jnp.float32,
    )
    return (maxima, totals, (summed / totals[..., None]).astype(jnp.bfloat16))


def merge_sources(partials, maxima, totals):
    highest = jnp.max(maxima, axis=0)
    shares = totals * jnp.exp(maxima - highest[None])
    summed = jnp.sum(shares, axis=0)
    numerator = jnp.sum(shares[..., None] * partials.astype(jnp.float32), axis=0)
    return (highest, summed, numerator / summed[..., None])


def merge_tuple(received):
    return merge_sources(received[0], received[1], received[2])


def join_pairs(earlier, later):
    highest = jnp.maximum(earlier[0], later[0])
    left_share = earlier[1] * jnp.exp(earlier[0] - highest)
    right_share = later[1] * jnp.exp(later[0] - highest)
    summed = left_share + right_share
    blended = (left_share[..., None] * earlier[2] + right_share[..., None] * later[2]) / summed[
        ..., None
    ]
    return (highest, summed, blended)


def absorb(query_nope, query_rope, key_weight):
    absorbed = jnp.einsum(
        "bqhn,hnd->bqhd", query_nope, key_weight, preferred_element_type=jnp.float32
    )
    return jnp.concatenate([absorbed.astype(jnp.bfloat16), query_rope], axis=-1)


def up_project(latent_out, value_weight):
    values = jnp.einsum(
        "bqhd,hde->bqhe", latent_out, value_weight, preferred_element_type=jnp.float32
    ).astype(jnp.bfloat16)
    return values.reshape(values.shape[0], values.shape[1], values.shape[2] * values.shape[3])


def shards(query_nope, query_rope, latent_cache, lengths, key_weight, value_weight, output_weight):
    latent_width = key_weight.shape[2]
    factor = float(query_nope.shape[3] + query_rope.shape[3]) ** (-0.5)
    positions = latent_cache.shape[1]
    drafts = query_nope.shape[1]
    offset = (lax.axis_index("seq") * lax.axis_size("grp") + lax.axis_index("grp")) * positions
    limits = lengths[:, None] - drafts + 1 + lax.broadcasted_iota(jnp.int32, (1, drafts), 1)
    own_queries = absorb(query_nope, query_rope, key_weight)
    maxima, totals, partials = shard_partial(
        lax.all_gather(own_queries, "seq", axis=2, tiled=True),
        latent_cache,
        limits,
        offset,
        factor,
        latent_width,
    )
    partials, maxima, totals = (partials, maxima, totals)
    sources = (partials[None], maxima[None], totals[None])
    gathered = merge_tuple(
        (
            lax.all_to_all(
                sources[0].astype(jnp.float32), "seq", split_axis=3, concat_axis=0, tiled=True
            ).astype(jnp.bfloat16),
            lax.all_to_all(sources[1], "seq", split_axis=3, concat_axis=0, tiled=True),
            lax.all_to_all(sources[2], "seq", split_axis=3, concat_axis=0, tiled=True),
        )
    )
    highest, summed, blended = joined((gathered[0], gathered[1], gathered[2]), "grp", join_pairs)
    values = up_project(blended.astype(jnp.bfloat16), value_weight)
    head_terms = jnp.dot(values, output_weight, preferred_element_type=jnp.float32)
    reduced = lax.psum_scatter(head_terms, "seq", scatter_dimension=2, tiled=True)
    return reduced.astype(jnp.bfloat16)


def solution(mesh):
    in_specs = (
        P(None, None, "seq", None),
        P(None, None, "seq", None),
        P(None, ("seq", "grp"), None),
        P(),
        P("seq", None, None),
        P("seq", None, None),
        P("seq", "grp"),
    )
    out_specs = P(None, None, ("grp", "seq"))
    return jax.shard_map(shards, mesh=mesh, in_specs=in_specs, out_specs=out_specs, check_vma=False)
```

profile of v0, /device:TPU:0, one launch (start us, length us, event | category | flops | bytes accessed | tf_op | source)
XLA Modules:
  0.0 212.3 jit_solution(17703678175560071938)
XLA Ops:
  8.1 1.1 fusion.18
  10.2 44.5 %all-gather.5.cloned.1.call-done = bf16[4,2,128,576]{3,0,1,2:T(4,128)(2,1)} async-done(((bf16[4,2,16,576]{3,0,1,2:T(4,128)(2,1)}), bf16[4,2,128,576]{3,0,1,2:T(4,128)(2,1)}) %all-gather.5.cloned.1.call-update) | async-done | bytes 1179664 | tf_op jit(solution)/shard_map/all_gather | solution.py:87
  54.7 2.4 %fusion.42 = (f32[4,2,128]{2,1,0:T(2,128)S(1)}, f32[4,2,128,256]{3,2,1,0:T(8,128)S(1)}) fusion(bf16[4,256,576]{1,2,0:T(8,128)(2,1)} %param.11, bf16[4,2,128,576]{3,0,1,2:T(4,128)(2,1)} %all-gather.5.cloned.1.call-done, pred[4,2,256]{2,1,0:T(4,128)(4,1)S(1)} %broadcast_compare_fusion), kind=kOutput, calls=%fused_computation.50 | convolution fusion | flops 302775296 | bytes 3414016 | tf_op jit(solution)/shard_map/bqhd,bpd->bqhp/dot_general | solution.py:22
  58.5 3.4 %all-to-all-start.1 = ((f32[8,1,128]{2,1,0:T(1,128)}), f32[8,1,128]{2,1,0:T(1,128)S(1)}, u32[]{:S(2)}, u32[]{:S(2)}) async-start(f32[8,1,128]{2,1,0:T(1,128)} %reshape.85), calls=%async_computation.1 | async-start | bytes 8192 | tf_op jit(solution)/shard_map/all_to_all | solution.py:102
  62.9 5.5 %all-to-all-done.1 = f32[8,1,128]{2,1,0:T(1,128)S(1)} async-done(((f32[8,1,128]{2,1,0:T(1,128)}), f32[8,1,128]{2,1,0:T(1,128)S(1)}, u32[]{:S(2)}, u32[]{:S(2)}) %all-to-all-start.1) | async-done | bytes 4128 | tf_op jit(solution)/shard_map/all_to_all | solution.py:102
  68.4 3.3 %all-to-all-start = ((f32[8,1,128]{2,1,0:T(1,128)}), f32[8,1,128]{2,1,0:T(1,128)S(1)}, u32[]{:S(2)}, u32[]{:S(2)}) async-start(f32[8,1,128]{2,1,0:T(1,128)} %reshape.83), calls=%async_computation | async-start | bytes 8192 | tf_op jit(solution)/shard_map/all_to_all | solution.py:101
  71.7 1.7 fusion.11
  73.5 2.1 copy.38
  75.6 2.5 %all-to-all-done = f32[8,1,128]{2,1,0:T(1,128)S(1)} async-done(((f32[8,1,128]{2,1,0:T(1,128)}), f32[8,1,128]{2,1,0:T(1,128)S(1)}, u32[]{:S(2)}, u32[]{:S(2)}) %all-to-all-start) | async-done | bytes 4128 | tf_op jit(solution)/shard_map/all_to_all | solution.py:101
  78.1 3.6 %all-to-all-start.2 = ((bf16[1,4,2,128,512]{4,2,1,0,3:T(2,128)(2,1)}), bf16[1,4,2,128,512]{4,2,1,0,3:T(2,128)(2,1)S(1)}, u32[]{:S(2)}, u32[]{:S(2)}) async-start(bf16[1,4,2,128,512]{4,2,1,0,3:T(2,128)(2,1)} %copy.38), calls=%async_computation.2 | async-start | bytes 2097152 | tf_op jit(solution)/shard_map/all_to_all | solution.py:98
  83.1 1.6 copy.35
  86.6 1.8 fusion.40
  88.4 16.5 %all-to-all-done.2 = bf16[1,4,2,128,512]{4,2,1,0,3:T(2,128)(2,1)S(1)} async-done(((bf16[1,4,2,128,512]{4,2,1,0,3:T(2,128)(2,1)}), bf16[1,4,2,128,512]{4,2,1,0,3:T(2,128)(2,1)S(1)}, u32[]{:S(2)}, u32[]{:S(2)}) %all-to-all-start.2) | async-done | bytes 1048608 | tf_op jit(solution)/shard_map/all_to_all | solution.py:98
  104.9 2.3 %fusion.7 = f32[4,2,16,512]{3,1,0,2:T(2,128)S(1)} fusion(bf16[1,4,2,8,16,512]{5,2,1,4,3,0:T(2,128)(2,1)S(1)} %bitcast.108, f32[8,4,2,16]{2,1,3,0:T(4,128)} %get-tuple-element.201), kind=kLoop, calls=%fused_computation.13 | loop fusion | flops 1507328 | bytes 1314816 | tf_op jit(solution)/shard_map/reduce_sum | solution.py:45
  108.5 5.2 %all-gather.1 = f32[16,2,16]{2,1,0:T(2,128)S(1)} all-gather(f32[4,2,16]{2,1,0:T(2,128)S(1)} %copy.36), channel_id=3, replica_groups=mesh['seq'=8,'grp'=4] {'grp'}, dimensions={0}, use_global_device_ids=true | all-gather | bytes 2560 | tf_op jit(solution)/shard_map/all_gather | solution.py:10
  113.7 5.2 %all-gather = f32[16,2,16]{2,1,0:T(2,128)S(1)} all-gather(f32[4,2,16]{2,1,0:T(2,128)S(1)} %copy.33), channel_id=2, replica_groups=mesh['seq'=8,'grp'=4] {'grp'}, dimensions={0}, use_global_device_ids=true | all-gather | bytes 2560 | tf_op jit(solution)/shard_map/all_gather | solution.py:10
  118.9 5.1 %all-gather.7.cloned.1.call-done = f32[4,4,2,16,512]{4,3,2,1,0:T(8,128)} async-done(((f32[1,4,2,16,512]{4,3,2,1,0:T(8,128)}), f32[4,4,2,16,512]{4,3,2,1,0:T(8,128)}) %all-gather.7.cloned.1.call-update) | async-done | bytes 1048592 | tf_op jit(solution)/shard_map/all_gather | solution.py:10
  124.9 3.5 %while.19 = (s32[]{:T(128)}, f32[4,2,16]{2,1,0:T(2,128)S(1)}, f32[4,2,16]{2,1,0:T(2,128)S(1)}, f32[4,2,16,512]{3,2,1,0:T(8,128)S(1)}, f32[4,4,2,16]{3,2,1,0:T(2,...) while((s32[]{:T(128)}, f32[4,2,16]{2,1,0:T(2,128)S(1)}, ...), condition=%wide.region_6.7_spmd, body=%wide.region_5.6_spmd.sunk | while | flops 262917 | bytes 792207 | solution.py:15
  125.0 1.1 fusion.46
  128.4 2.0 fusion.24
  130.5 4.2 %fusion.3 = f32[4,2,1792]{2,0,1:T(4,128)S(1)} fusion(bf16[2048,1792]{1,0:T(8,128)(2,1)} %param.15, bf16[16,2,1,4,128]{4,3,2,1,0:T(4,128)(2,1)S(1)} %fusion.24), kind=kOutput, calls=%fused_computation.8 | convolution fusion | flops 58720256 | bytes 7430144 | tf_op jit(solution)/shard_map/dot_general | solution.py:107
  134.7 2.3 %copy.49 = f32[4,2,1792]{0,1,2:T(2,128)} copy(f32[4,2,1792]{2,0,1:T(4,128)S(1)} %fusion.3) | data formatting | bytes 114688
  137.0 3.1 %reshape.81 = f32[1792,8]{1,0:T(8,128)} reshape(f32[1792,2,4]{2,1,0:T(2,128)} %bitcast.107) | data formatting | bytes 114688
  140.1 63.9 %reduce-scatter.4.cloned.1.call-done = f32[224,8]{1,0:T(8,128)} async-done(((f32[1792,8]{1,0:T(8,128)}), f32[224,8]{1,0:T(8,128)}) %reduce-scatter.4.cloned.1.call-update) | async-done | bytes 7184
  (44 shorter events, 14.4 us)
Async XLA Ops:
  6.5 1.6 copy-start
  6.5 3.5 %copy-start.1 = (s32[4]{0:T(128)S(1)}, s32[4]{0:T(128)}, u32[]{:S(2)}) copy-start(s32[4]{0:T(128)} %param.12) | copy-start | bytes 52
  6.5 48.2 %all-gather.5.cloned.1.call-start = ((), (), s32[]{:S(2)}) async-start(), calls=%async_computation.4 | async-start | bytes 1474560 | tf_op jit(solution)/shard_map/all_gather | solution.py:87
  58.5 9.9 %all-to-all-start.1 = ((f32[8,1,128]{2,1,0:T(1,128)}), f32[8,1,128]{2,1,0:T(1,128)S(1)}, u32[]{:S(2)}, u32[]{:S(2)}) async-start(f32[8,1,128]{2,1,0:T(1,128)} %reshape.85), calls=%async_computation.1 | async-start | bytes 8192 | tf_op jit(solution)/shard_map/all_to_all | solution.py:102
  68.4 9.7 %all-to-all-start = ((f32[8,1,128]{2,1,0:T(1,128)}), f32[8,1,128]{2,1,0:T(1,128)S(1)}, u32[]{:S(2)}, u32[]{:S(2)}) async-start(f32[8,1,128]{2,1,0:T(1,128)} %reshape.83), calls=%async_computation | async-start | bytes 8192 | tf_op jit(solution)/shard_map/all_to_all | solution.py:101
  78.1 26.8 %all-to-all-start.2 = ((bf16[1,4,2,128,512]{4,2,1,0,3:T(2,128)(2,1)}), bf16[1,4,2,128,512]{4,2,1,0,3:T(2,128)(2,1)S(1)}, u32[]{:S(2)}, u32[]{:S(2)}) async-start(bf16[1,4,2,128,512]{4,2,1,0,3:T(2,128)(2,1)} %copy.38), calls=%async_computation.2 | async-start | bytes 2097152 | tf_op jit(solution)/shard_map/all_to_all | solution.py:98
  81.6 42.3 %all-gather.7.cloned.1.call-start = ((), (), s32[]{:S(2)}) async-start(), calls=%async_computation.5 | async-start | bytes 1310720 | tf_op jit(solution)/shard_map/all_gather | solution.py:10
  108.2 95.8 %reduce-scatter.4.cloned.1.call-start = ((), (), s32[]{:S(2)}) async-start(), calls=%async_computation.6 | async-start | bytes 1032192
Sparse Core Ops, SparseCore 0:
  10.2 44.5 all-gather.4
  108.4 15.5 all-gather.6
  140.3 63.6 reduce-scatter.3
where the time goes:
time: 213 us; the launch traced here: 212 us
  waiting for transfers between devices  138 us (65%)
  local copies, waits for them, and re-layouts  18.2 us (9%)
  between operations  13.3 us (6%)
  matrix products  11.5 us (5%)
  starting transfers between devices  10.4 us (5%)
  blocking collectives  10.4 us (5%)
  other arithmetic  10.3 us (5%)
    unnamed x4, waiting for transfers between devices  63.9 us
    all_gather x1, waiting for transfers between devices, shards(): lax.all_gather(own_queries, 'seq', axis=2, tiled=True)  44.5 us
    all_to_all x1, waiting for transfers between devices, shards(): lax.all_to_all(sources[0].astype(jnp.float32), 'seq', split_axis=3, conca...  16.5 us
    all_gather x2, blocking collectives, joined(): gathered = jax.tree.map(lambda a: lax.all_gather(a, axis), part)  10.4 us
    unnamed x13, local copies, waits for them, and re-layouts  10.2 us
    all_to_all x1, waiting for transfers between devices, shards(): lax.all_to_all(sources[2], 'seq', split_axis=3, concat_axis=0, tiled=True)  5.53 us
    all_gather x1, waiting for transfers between devices, joined(): gathered = jax.tree.map(lambda a: lax.all_gather(a, axis), part)  5.1 us
  transfers between devices with their start and end apart: 6, of which 6 were waited for; matrix products, arithmetic and copies ran while one was open for 6% of the time, Pallas kernels for 0%

commit v1 on v0

--- a/solution.py
+++ b/solution.py
@@ -4,6 +4,19 @@
 from jax.sharding import PartitionSpec as P
 
 NEGATIVE = -1e30
+
+
+def collect(x, axis, dim):
+    ways = lax.axis_size(axis)
+    up = [(d, (d + 1) % ways) for d in range(ways)]
+    down = [(d, (d - 1) % ways) for d in range(ways)]
+    earlier, later = ([x], [x])
+    for _ in range(ways // 2):
+        earlier.append(lax.ppermute(earlier[-1], axis, up))
+    for _ in range((ways - 1) // 2):
+        later.append(lax.ppermute(later[-1], axis, down))
+    line = jnp.concatenate([*earlier[::-1], *later[1:]], axis=dim)
+    return jnp.roll(line, (lax.axis_index(axis) - ways // 2) * x.shape[dim], axis=dim)
 
 
 def joined(part, axis, combine):
@@ -84,12 +97,7 @@
     limits = lengths[:, None] - drafts + 1 + lax.broadcasted_iota(jnp.int32, (1, drafts), 1)
     own_queries = absorb(query_nope, query_rope, key_weight)
     maxima, totals, partials = shard_partial(
-        lax.all_gather(own_queries, "seq", axis=2, tiled=True),
-        latent_cache,
-        limits,
-        offset,
-        factor,
-        latent_width,
+        collect(own_queries, "seq", 2), latent_cache, limits, offset, factor, latent_width
     )
     partials, maxima, totals = (partials, maxima, totals)
     sources = (partials[None], maxima[None], totals[None])

time: 213 us -> 201 us (0.944)
  waiting for transfers between devices: 138 us -> 105 us
  starting transfers between devices: 10.4 us -> 30.8 us
    all_gather x1 -> x0, waiting for transfers between devices: 44.5 us -> none  [shards(): lax.all_gather(own_queries, 'seq', axis=2, tiled=True)]
    ppermute x0 -> x7, starting transfers between devices: none -> 18.3 us  [the longest x3 12 us: collect(): later.append(lax.ppermute(later[-1], axis, down))]
    ppermute x0 -> x7, waiting for transfers between devices: none -> 17.7 us  [the longest x4 17.7 us: collect(): earlier.append(lax.ppermute(earlier[-1], axis, up))]
    all_to_all x1, waiting for transfers between devices: 16.5 us -> 11.1 us  [shards(): lax.all_to_all(sources[0].astype(jnp.float32), 'seq', split_axis=3, conca...]
    all_to_all x1, waiting for transfers between devices: 5.53 us -> 2.73 us  [shards(): lax.all_to_all(sources[2], 'seq', split_axis=3, concat_axis=0, tiled=True)]
    all_to_all x1, waiting for transfers between devices: 2.53 us -> 5.06 us  [shards(): lax.all_to_all(sources[1], 'seq', split_axis=3, concat_axis=0, tiled=True)]
    all_to_all x1, starting transfers between devices: 3.31 us -> 5.53 us  [shards(): lax.all_to_all(sources[1], 'seq', split_axis=3, concat_axis=0, tiled=True)]
    unnamed x13 -> x28, local copies, waits for them, and re-layouts: 10.2 us -> 11.3 us
  transfers between devices with their start and end apart: 6 -> 12, of which waited for: 6 -> 9; matrix products, arithmetic and copies ran while one was open for 6% -> 6% of each run, Pallas kernels for 0% -> 0%
where the time goes in v1:
time: 201 us; the launch traced here: 200 us
  waiting for transfers between devices  105 us (52%)
  starting transfers between devices  30.8 us (15%)
  local copies, waits for them, and re-layouts  19.8 us (10%)
  between operations  13.7 us (7%)
  blocking collectives  10.6 us (5%)
  other arithmetic  9.85 us (5%)
  matrix products  9.81 us (5%)
    unnamed x3, waiting for transfers between devices  63.9 us
    ppermute x4, waiting for transfers between devices, collect(): earlier.append(lax.ppermute(earlier[-1], axis, up))  17.7 us
    ppermute x3, starting transfers between devices, collect(): later.append(lax.ppermute(later[-1], axis, down))  12 us
    unnamed x28, local copies, waits for them, and re-layouts  11.3 us
    all_to_all x1, waiting for transfers between devices, shards(): lax.all_to_all(sources[0].astype(jnp.float32), 'seq', split_axis=3, conca...  11.1 us
    all_gather x2, blocking collectives, joined(): gathered = jax.tree.map(lambda a: lax.all_gather(a, axis), part)  10.6 us
    ppermute x4, starting transfers between devices, collect(): earlier.append(lax.ppermute(earlier[-1], axis, up))  6.29 us
    all_to_all x1, starting transfers between devices, shards(): lax.all_to_all(sources[1], 'seq', split_axis=3, concat_axis=0, tiled=True)  5.53 us
  transfers between devices with their start and end apart: 12, of which 9 were waited for; matrix products, arithmetic and copies ran while one was open for 6% of the time, Pallas kernels for 0%

profile of v1, /device:TPU:0, one launch (start us, length us, event | category | flops | bytes accessed | tf_op | source)
XLA Modules:
  0.0 200.0 jit_solution(7288513586070747988)
XLA Ops:
  9.4 3.0 %collective-permute-start = (bf16[4,2,16,576]{3,0,1,2:T(4,128)(2,1)S(1)}, bf16[4,2,16,576]{3,0,1,2:T(4,128)(2,1)S(1)}, u32[]{:S(2)}, u32[]{:S(2)}) collective-permute-start(bf16[4,2,16,576]{3,0,1,2:T(4,128)(2,1)S(1)} %pad_maximum_fusion), channel_id=1, source_target_pairs={{0,4},{4,8},{8,12},{12,16},{16,20},{20,24},{24,28},{28,0},{1,5},{5... | collective-permute-start | bytes 442376 | tf_op jit(solution)/shard_map/ppermute | solution.py:15
  12.4 3.1 %collective-permute-start.4 = (bf16[4,2,16,576]{3,0,1,2:T(4,128)(2,1)S(1)}, bf16[4,2,16,576]{3,0,1,2:T(4,128)(2,1)S(1)}, u32[]{:S(2)}, u32[]{:S(2)}) collective-permute-start(bf16[4,2,16,576]{3,0,1,2:T(4,128)(2,1)S(1)} %pad_maximum_fusion), channel_id=1, source_target_pairs={{0,28},{4,0},{8,4},{12,8},{16,12},{20,16},{24,20},{28,24},{1,29},{... | collective-permute-start | bytes 442376 | tf_op jit(solution)/shard_map/ppermute | solution.py:17
  15.5 4.2 %collective-permute-done = bf16[4,2,16,576]{3,0,1,2:T(4,128)(2,1)S(1)} collective-permute-done((bf16[4,2,16,576]{3,0,1,2:T(4,128)(2,1)S(1)}, bf16[4,2,16,576]{3,0,1,2:T(4,128)(2,1)S(1)}, u32[]{:S(2)}, u32[]{:S(2)}) %collective-permute-start) | collective-permute-done | bytes 147488 | tf_op jit(solution)/shard_map/ppermute | solution.py:15
  19.8 2.1 %collective-permute-start.1 = (bf16[4,2,16,576]{3,0,1,2:T(4,128)(2,1)S(1)}, bf16[4,2,16,576]{3,0,1,2:T(4,128)(2,1)S(1)}, u32[]{:S(2)}, u32[]{:S(2)}) collective-permute-start(bf16[4,2,16,576]{3,0,1,2:T(4,128)(2,1)S(1)} %collective-permute-done), channel_id=1, source_target_pairs={{0,4},{4,8},{8,12},{12,16},{16,20},{20,24},{24,28},{28,0},{1,5},{5... | collective-permute-start | bytes 442376 | tf_op jit(solution)/shard_map/ppermute | solution.py:15
  21.9 7.0 %collective-permute-done.1 = bf16[4,2,16,576]{3,0,1,2:T(4,128)(2,1)S(1)} collective-permute-done((bf16[4,2,16,576]{3,0,1,2:T(4,128)(2,1)S(1)}, bf16[4,2,16,576]{3,0,1,2:T(4,128)(2,1)S(1)}, u32[]{:S(2)}, u32[]{:S(2)}) %collective-permute-start.1) | collective-permute-done | bytes 147488 | tf_op jit(solution)/shard_map/ppermute | solution.py:15
  29.0 4.7 %collective-permute-start.5 = (bf16[4,2,16,576]{3,0,1,2:T(4,128)(2,1)S(1)}, bf16[4,2,16,576]{3,0,1,2:T(4,128)(2,1)S(1)}, u32[]{:S(2)}, u32[]{:S(2)}) collective-permute-start(bf16[4,2,16,576]{3,0,1,2:T(4,128)(2,1)S(1)} %collective-permute-done.4), channel_id=1, source_target_pairs={{0,28},{4,0},{8,4},{12,8},{16,12},{20,16},{24,20},{28,24},{1,29},{... | collective-permute-start | bytes 442376 | tf_op jit(solution)/shard_map/ppermute | solution.py:17
  33.7 3.3 %collective-permute-done.2 = bf16[4,2,16,576]{3,0,1,2:T(4,128)(2,1)S(1)} collective-permute-done((bf16[4,2,16,576]{3,0,1,2:T(4,128)(2,1)S(1)}, bf16[4,2,16,576]{3,0,1,2:T(4,128)(2,1)S(1)}, u32[]{:S(2)}, u32[]{:S(2)}) %collective-permute-start.2) | collective-permute-done | bytes 147488 | tf_op jit(solution)/shard_map/ppermute | solution.py:15
  38.2 4.2 %collective-permute-start.6 = (bf16[4,2,16,576]{3,0,1,2:T(4,128)(2,1)S(1)}, bf16[4,2,16,576]{3,0,1,2:T(4,128)(2,1)S(1)}, u32[]{:S(2)}, u32[]{:S(2)}) collective-permute-start(bf16[4,2,16,576]{3,0,1,2:T(4,128)(2,1)S(1)} %collective-permute-done.5), channel_id=1, source_target_pairs={{0,28},{4,0},{8,4},{12,8},{16,12},{20,16},{24,20},{28,24},{1,29},{... | collective-permute-start | bytes 442376 | tf_op jit(solution)/shard_map/ppermute | solution.py:17
  42.4 3.2 %collective-permute-done.3 = bf16[4,2,16,576]{3,0,1,2:T(4,128)(2,1)S(1)} collective-permute-done((bf16[4,2,16,576]{3,0,1,2:T(4,128)(2,1)S(1)}, bf16[4,2,16,576]{3,0,1,2:T(4,128)(2,1)S(1)}, u32[]{:S(2)}, u32[]{:S(2)}) %collective-permute-start.3) | collective-permute-done | bytes 147488 | tf_op jit(solution)/shard_map/ppermute | solution.py:15
  49.2 5.5 %all-to-all-start = ((f32[8,1,128]{2,1,0:T(1,128)}), f32[8,1,128]{2,1,0:T(1,128)S(1)}, u32[]{:S(2)}, u32[]{:S(2)}) async-start(f32[8,1,128]{2,1,0:T(1,128)} %reshape.83), calls=%async_computation | async-start | bytes 8192 | tf_op jit(solution)/shard_map/all_to_all | solution.py:109
  56.1 5.1 %all-to-all-done = f32[8,1,128]{2,1,0:T(1,128)S(1)} async-done(((f32[8,1,128]{2,1,0:T(1,128)}), f32[8,1,128]{2,1,0:T(1,128)S(1)}, u32[]{:S(2)}, u32[]{:S(2)}) %all-to-all-start) | async-done | bytes 4128 | tf_op jit(solution)/shard_map/all_to_all | solution.py:109
  61.2 3.3 %all-to-all-start.1 = ((f32[8,1,128]{2,1,0:T(1,128)}), f32[8,1,128]{2,1,0:T(1,128)S(1)}, u32[]{:S(2)}, u32[]{:S(2)}) async-start(f32[8,1,128]{2,1,0:T(1,128)} %reshape.85), calls=%async_computation.1 | async-start | bytes 8192 | tf_op jit(solution)/shard_map/all_to_all | solution.py:110
  68.3 2.7 %all-to-all-done.1 = f32[8,1,128]{2,1,0:T(1,128)S(1)} async-done(((f32[8,1,128]{2,1,0:T(1,128)}), f32[8,1,128]{2,1,0:T(1,128)S(1)}, u32[]{:S(2)}, u32[]{:S(2)}) %all-to-all-start.1) | async-done | bytes 4128 | tf_op jit(solution)/shard_map/all_to_all | solution.py:110
  71.0 3.6 %all-to-all-start.2 = ((bf16[1,4,2,128,512]{4,2,1,0,3:T(2,128)(2,1)}), bf16[1,4,2,128,512]{4,2,1,0,3:T(2,128)(2,1)S(1)}, u32[]{:S(2)}, u32[]{:S(2)}) async-start(bf16[1,4,2,128,512]{4,2,1,0,3:T(2,128)(2,1)} %copy.44), calls=%async_computation.2 | async-start | bytes 2097152 | tf_op jit(solution)/shard_map/all_to_all | solution.py:106
  81.3 11.1 %all-to-all-done.2 = bf16[1,4,2,128,512]{4,2,1,0,3:T(2,128)(2,1)S(1)} async-done(((bf16[1,4,2,128,512]{4,2,1,0,3:T(2,128)(2,1)}), bf16[1,4,2,128,512]{4,2,1,0,3:T(2,128)(2,1)S(1)}, u32[]{:S(2)}, u32[]{:S(2)}) %all-to-all-start.2) | async-done | bytes 1048608 | tf_op jit(solution)/shard_map/all_to_all | solution.py:106
  92.4 2.3 %fusion.7 = f32[4,2,16,512]{3,1,0,2:T(2,128)S(1)} fusion(bf16[1,4,2,8,16,512]{5,2,1,4,3,0:T(2,128)(2,1)S(1)} %bitcast.108, f32[8,4,2,16]{2,1,3,0:T(4,128)} %get-tuple-element.201), kind=kLoop, calls=%fused_computation.13 | loop fusion | flops 1507328 | bytes 1314816 | tf_op jit(solution)/shard_map/reduce_sum | solution.py:58
  96.0 5.2 %all-gather = f32[16,2,16]{2,1,0:T(2,128)S(1)} all-gather(f32[4,2,16]{2,1,0:T(2,128)S(1)} %copy.39), channel_id=2, replica_groups=mesh['seq'=8,'grp'=4] {'grp'}, dimensions={0}, use_global_device_ids=true | all-gather | bytes 2560 | tf_op jit(solution)/shard_map/all_gather | solution.py:23
  101.2 5.4 %all-gather.1 = f32[16,2,16]{2,1,0:T(2,128)S(1)} all-gather(f32[4,2,16]{2,1,0:T(2,128)S(1)} %copy.42), channel_id=3, replica_groups=mesh['seq'=8,'grp'=4] {'grp'}, dimensions={0}, use_global_device_ids=true | all-gather | bytes 2560 | tf_op jit(solution)/shard_map/all_gather | solution.py:23
  106.6 4.8 %all-gather.4.cloned.1.call-done = f32[4,4,2,16,512]{4,3,2,1,0:T(8,128)} async-done(((f32[1,4,2,16,512]{4,3,2,1,0:T(8,128)}), f32[4,4,2,16,512]{4,3,2,1,0:T(8,128)}) %all-gather.4.cloned.1.call-update) | async-done | bytes 1048592 | tf_op jit(solution)/shard_map/all_gather | solution.py:23
  112.4 3.5 %while.19 = (s32[]{:T(128)}, f32[4,2,16]{2,1,0:T(2,128)S(1)}, f32[4,2,16]{2,1,0:T(2,128)S(1)}, f32[4,2,16,512]{3,2,1,0:T(8,128)S(1)}, f32[4,4,2,16]{3,2,1,0:T(2,...) while((s32[]{:T(128)}, f32[4,2,16]{2,1,0:T(2,128)S(1)}, ...), condition=%wide.region_6.7_spmd, body=%wide.region_5.6_spmd.sunk | while | flops 262917 | bytes 792215 | solution.py:28
  117.9 4.2 %fusion.3 = f32[4,2,1792]{2,0,1:T(4,128)S(1)} fusion(bf16[2048,1792]{1,0:T(8,128)(2,1)} %param.15, bf16[16,2,1,4,128]{4,3,2,1,0:T(4,128)(2,1)S(1)} %fusion.24), kind=kOutput, calls=%fused_computation.8 | convolution fusion | flops 58720256 | bytes 7430144 | tf_op jit(solution)/shard_map/dot_general | solution.py:115
  122.1 2.3 %copy.55 = f32[4,2,1792]{0,1,2:T(2,128)} copy(f32[4,2,1792]{2,0,1:T(4,128)S(1)} %fusion.3) | data formatting | bytes 114688
  124.4 3.1 %reshape.81 = f32[1792,8]{1,0:T(8,128)} reshape(f32[1792,2,4]{2,1,0:T(2,128)} %bitcast.107) | data formatting | bytes 114688
  127.6 63.9 %reduce-scatter.4.cloned.1.call-done = f32[224,8]{1,0:T(8,128)} async-done(((f32[1792,8]{1,0:T(8,128)}), f32[224,8]{1,0:T(8,128)}) %reduce-scatter.4.cloned.1.call-update) | async-done | bytes 7184
  (74 shorter events, 28.8 us)
Async XLA Ops:
  6.5 1.6 copy-start
  6.5 15.3 %copy-start.2 = (s32[4]{0:T(128)S(1)}, s32[4]{0:T(128)}, u32[]{:S(2)}) copy-start(s32[4]{0:T(128)} %param.12) | copy-start | bytes 52
  9.4 10.4 %collective-permute-start = (bf16[4,2,16,576]{3,0,1,2:T(4,128)(2,1)S(1)}, bf16[4,2,16,576]{3,0,1,2:T(4,128)(2,1)S(1)}, u32[]{:S(2)}, u32[]{:S(2)}) collective-permute-start(bf16[4,2,16,576]{3,0,1,2:T(4,128)(2,1)S(1)} %pad_maximum_fusion), channel_id=1, source_target_pairs={{0,4},{4,8},{8,12},{12,16},{16,20},{20,24},{24,28},{28,0},{1,5},{5... | collective-permute-start | bytes 442376 | tf_op jit(solution)/shard_map/ppermute | solution.py:15
  12.4 16.6 %collective-permute-start.4 = (bf16[4,2,16,576]{3,0,1,2:T(4,128)(2,1)S(1)}, bf16[4,2,16,576]{3,0,1,2:T(4,128)(2,1)S(1)}, u32[]{:S(2)}, u32[]{:S(2)}) collective-permute-start(bf16[4,2,16,576]{3,0,1,2:T(4,128)(2,1)S(1)} %pad_maximum_fusion), channel_id=1, source_target_pairs={{0,28},{4,0},{8,4},{12,8},{16,12},{20,16},{24,20},{28,24},{1,29},{... | collective-permute-start | bytes 442376 | tf_op jit(solution)/shard_map/ppermute | solution.py:17
  19.8 9.1 %collective-permute-start.1 = (bf16[4,2,16,576]{3,0,1,2:T(4,128)(2,1)S(1)}, bf16[4,2,16,576]{3,0,1,2:T(4,128)(2,1)S(1)}, u32[]{:S(2)}, u32[]{:S(2)}) collective-permute-start(bf16[4,2,16,576]{3,0,1,2:T(4,128)(2,1)S(1)} %collective-permute-done), channel_id=1, source_target_pairs={{0,4},{4,8},{8,12},{12,16},{16,20},{20,24},{24,28},{28,0},{1,5},{5... | collective-permute-start | bytes 442376 | tf_op jit(solution)/shard_map/ppermute | solution.py:15
  28.9 8.1 %collective-permute-start.2 = (bf16[4,2,16,576]{3,0,1,2:T(4,128)(2,1)S(1)}, bf16[4,2,16,576]{3,0,1,2:T(4,128)(2,1)S(1)}, u32[]{:S(2)}, u32[]{:S(2)}) collective-permute-start(bf16[4,2,16,576]{3,0,1,2:T(4,128)(2,1)S(1)} %collective-permute-done.1), channel_id=1, source_target_pairs={{0,4},{4,8},{8,12},{12,16},{16,20},{20,24},{24,28},{28,0},{1,5},{5... | collective-permute-start | bytes 442376 | tf_op jit(solution)/shard_map/ppermute | solution.py:15
  29.0 9.2 %collective-permute-start.5 = (bf16[4,2,16,576]{3,0,1,2:T(4,128)(2,1)S(1)}, bf16[4,2,16,576]{3,0,1,2:T(4,128)(2,1)S(1)}, u32[]{:S(2)}, u32[]{:S(2)}) collective-permute-start(bf16[4,2,16,576]{3,0,1,2:T(4,128)(2,1)S(1)} %collective-permute-done.4), channel_id=1, source_target_pairs={{0,28},{4,0},{8,4},{12,8},{16,12},{20,16},{24,20},{28,24},{1,29},{... | collective-permute-start | bytes 442376 | tf_op jit(solution)/shard_map/ppermute | solution.py:17
  37.0 8.6 %collective-permute-start.3 = (bf16[4,2,16,576]{3,0,1,2:T(4,128)(2,1)S(1)}, bf16[4,2,16,576]{3,0,1,2:T(4,128)(2,1)S(1)}, u32[]{:S(2)}, u32[]{:S(2)}) collective-permute-start(bf16[4,2,16,576]{3,0,1,2:T(4,128)(2,1)S(1)} %collective-permute-done.2), channel_id=1, source_target_pairs={{0,4},{4,8},{8,12},{12,16},{16,20},{20,24},{24,28},{28,0},{1,5},{5... | collective-permute-start | bytes 442376 | tf_op jit(solution)/shard_map/ppermute | solution.py:15
  38.2 7.9 %collective-permute-start.6 = (bf16[4,2,16,576]{3,0,1,2:T(4,128)(2,1)S(1)}, bf16[4,2,16,576]{3,0,1,2:T(4,128)(2,1)S(1)}, u32[]{:S(2)}, u32[]{:S(2)}) collective-permute-start(bf16[4,2,16,576]{3,0,1,2:T(4,128)(2,1)S(1)} %collective-permute-done.5), channel_id=1, source_target_pairs={{0,28},{4,0},{8,4},{12,8},{16,12},{20,16},{24,20},{28,24},{1,29},{... | collective-permute-start | bytes 442376 | tf_op jit(solution)/shard_map/ppermute | solution.py:17
  46.3 1.3 copy-start.1
  49.2 12.0 %all-to-all-start = ((f32[8,1,128]{2,1,0:T(1,128)}), f32[8,1,128]{2,1,0:T(1,128)S(1)}, u32[]{:S(2)}, u32[]{:S(2)}) async-start(f32[8,1,128]{2,1,0:T(1,128)} %reshape.83), calls=%async_computation | async-start | bytes 8192 | tf_op jit(solution)/shard_map/all_to_all | solution.py:109
  61.2 9.9 %all-to-all-start.1 = ((f32[8,1,128]{2,1,0:T(1,128)}), f32[8,1,128]{2,1,0:T(1,128)S(1)}, u32[]{:S(2)}, u32[]{:S(2)}) async-start(f32[8,1,128]{2,1,0:T(1,128)} %reshape.85), calls=%async_computation.1 | async-start | bytes 8192 | tf_op jit(solution)/shard_map/all_to_all | solution.py:110
  71.0 21.4 %all-to-all-start.2 = ((bf16[1,4,2,128,512]{4,2,1,0,3:T(2,128)(2,1)}), bf16[1,4,2,128,512]{4,2,1,0,3:T(2,128)(2,1)S(1)}, u32[]{:S(2)}, u32[]{:S(2)}) async-start(bf16[1,4,2,128,512]{4,2,1,0,3:T(2,128)(2,1)} %copy.44), calls=%async_computation.2 | async-start | bytes 2097152 | tf_op jit(solution)/shard_map/all_to_all | solution.py:106
  74.6 36.8 %all-gather.4.cloned.1.call-start = ((), (), s32[]{:S(2)}) async-start(), calls=%async_computation.4 | async-start | bytes 1310720 | tf_op jit(solution)/shard_map/all_gather | solution.py:23
  95.7 95.7 %reduce-scatter.4.cloned.1.call-start = ((), (), s32[]{:S(2)}) async-start(), calls=%async_computation.5 | async-start | bytes 1032192
Sparse Core Ops, SparseCore 0:
  95.9 15.5 all-gather.3
  127.7 63.7 reduce-scatter.3
